TPU v7x, 32 devices: a whole 2x2x4 slice. The times are simulated.
32 devices in a mesh: group: 2 (over y), expert: 4 (over x, core), tensor: 4 (over z).
Axes of the slice: x: 2, y: 2, z: 4, core: 2. Of those that a mesh axis runs over, the one named last changes fastest.
Arguments:
- tokens: bfloat16 [512, 4096], P(('group', 'expert'), 'tensor'), parts along dimension 0, may hold values from -6 to 6
- w_gate: bfloat16 [8, 4096, 1536], P('expert', 'tensor'), may hold values from -0.125 to 0.125
- w_up: bfloat16 [8, 4096, 1536], P('expert', 'tensor'), may hold values from -0.125 to 0.125
- w_down: bfloat16 [8, 1536, 4096], P('expert', None, 'tensor'), may hold values from -0.15625 to 0.15625
- expert_ids: int32 [512, 8], P(('group', 'expert')), parts along dimension 0, may hold values from 0 to 7, as said below
- route_weights: float32 [512, 8], P(('group', 'expert')), parts along dimension 0, may hold values from 0.05 to 0.5
Outputs:
- mixed_out: bfloat16 [512, 4096], P(('group', 'expert'), 'tensor'), parts along dimension 0
There are 2 independent parts, one for each index of `group`. A program takes and returns all parts, laid end to end along the dimension named above; an argument that names none is the same for every part. Nothing has to cross between parts.
Inputs may be any that keep to these rules, and one draw needn't show every extreme that they name: `expert_ids`: each row names 8 different experts. In each aligned block of 64 rows no expert is named by more than 64 rows, and one expert, the same in every block of a part, is named by exactly 64 rows of every block.
All inputs are finite; a program needn't handle non-finite values.
Results may differ from a plain program's by a relative error of at most 0.0057.
Values may be sent and summed in bfloat16 or wider, within the bound.
A program may use at most 128 MiB of HBM per device.

v0:
```python
import jax
import jax.numpy as jnp
from jax import lax
from jax.sharding import PartitionSpec as P


def slot_numbers(flat_ids, experts_all):
    labels = jnp.arange(experts_all, dtype=jnp.int32)
    onehot = (flat_ids[:, None] == labels[None, :]).astype(jnp.int32)
    before = jnp.cumsum(onehot, axis=0) - onehot
    return jnp.sum(before * onehot, axis=1)


def per_device(tokens, w_gate, w_up, w_down, expert_ids, route_weights):
    n_expert = lax.axis_size("expert")
    held_experts = w_gate.shape[0]
    experts_all = held_experts * n_expert
    tok_rows = tokens.shape[0]
    col_share = tokens.shape[1]
    per_token = expert_ids.shape[1]
    capacity = min(tok_rows, 2 * tok_rows * per_token // experts_all)
    flat_ids = expert_ids.reshape(tok_rows * per_token)
    position = flat_ids * capacity + slot_numbers(flat_ids, experts_all)
    owners = jnp.arange(tok_rows * per_token, dtype=jnp.int32) // per_token
    source = jnp.full((experts_all * capacity,), -1, jnp.int32).at[position].set(owners)
    filled = (source >= 0)[:, None]
    picked_rows = jnp.where(filled, tokens[jnp.maximum(source, 0)], jnp.zeros((), tokens.dtype))
    outgoing = picked_rows.reshape(n_expert, held_experts, capacity, col_share)
    received = lax.all_to_all(outgoing, "expert", split_axis=0, concat_axis=0, tiled=True)
    gate_part = jnp.einsum("sjnd,jdf->sjnf", received, w_gate, preferred_element_type=jnp.float32)
    up_part = jnp.einsum("sjnd,jdf->sjnf", received, w_up, preferred_element_type=jnp.float32)
    gate_share = lax.psum_scatter(gate_part, "tensor", scatter_dimension=3, tiled=True)
    up_share = lax.psum_scatter(up_part, "tensor", scatter_dimension=3, tiled=True)
    hidden_share = (jax.nn.silu(gate_share) * up_share).astype(jnp.bfloat16)
    hidden = lax.all_gather(hidden_share, "tensor", axis=3, tiled=True)
    result = jnp.einsum("sjnf,jfd->sjnd", hidden, w_down, preferred_element_type=jnp.float32)
    returned = result.astype(jnp.bfloat16)
    combined = lax.all_to_all(returned, "expert", split_axis=0, concat_axis=0, tiled=True).reshape(
        experts_all * capacity, col_share
    )
    picked = combined[position].reshape(tok_rows, per_token, col_share).astype(jnp.float32)
    mixed_out = jnp.sum(picked * route_weights[:, :, None], axis=1)
    return mixed_out.astype(jnp.bfloat16)


def solution(mesh):
    in_specs = (
        P(("group", "expert"), "tensor"),
        P("expert", "tensor", None),
        P("expert", "tensor", None),
        P("expert", None, "tensor"),
        P(("group", "expert"), None),
        P(("group", "expert"), None),
    )
    out_specs = P(("group", "expert"), "tensor")
    return jax.shard_map(
        per_device, mesh=mesh, in_specs=in_specs, out_specs=out_specs, check_vma=False
    )
```

profile of v0, /device:TPU:0, one launch (start us, length us, event | category | flops | bytes accessed | tf_op | source)
XLA Modules:
  0.0 236.0 jit_solution(6427868677075579159)
XLA Ops:
  6.5 0.0 copy-start
  6.5 0.0 reduce-scatter.3.cloned.1.call-start
  6.5 0.8 copy.16
  7.3 0.1 eq.29
  7.4 0.1 eq.25
  7.5 0.7 broadcast_multiply_fusion
  8.2 1.1 reduce-window.6
  9.4 0.2 slice_reduce_fusion
  9.6 0.1 copy.15
  9.7 0.1 mul.32
  9.8 0.1 fusion.22
  9.9 2.4 %scatter_custom_fusion = s32[512]{0:T(512)S(1)} fusion(s32[512]{0:T(512)S(1)} %bitcast.47, s32[512]{0:T(512)S(1)} %add_select_fusion, s32[]{:T(128)} %constant.27.clone.1), kind=kCustom, calls=%fused_computation.39 | custom fusion | bytes 2052 | tf_op jit(solution)/shard_map/scatter | solution.py:25
  12.4 0.1 broadcast_in_dim.26
  12.5 0.0 copy-done
  12.5 2.1 gather_fusion
  14.5 0.1 broadcast_select_fusion
  14.7 18.5 %all_to_all.10 = bf16[4,2,64,1024]{3,2,1,0:T(8,128)(2,1)S(1)} all-to-all(bf16[4,2,64,1024]{3,2,1,0:T(8,128)(2,1)S(1)} %broadcast_select_fusion), channel_id=1, replica_groups=mesh['group'=2,'expert'=4,'tensor'=4] {'expert'}, dimensions={0} | all-to-all | bytes 2097152 | tf_op jit(solution)/shard_map/all_to_all | solution.py:29
  33.2 6.3 %fusion.6 = f32[4,2,64,1536]{3,2,0,1:T(8,128)} fusion(bf16[2,1024,1536]{2,1,0:T(8,128)(2,1)} %param.7, bf16[4,2,64,1024]{3,2,1,0:T(8,128)(2,1)S(1)} %all_to_all.10), kind=kOutput, calls=%fused_computation.9 | convolution fusion | flops 1610612736 | bytes 10485760 | tf_op jit(solution)/shard_map/sjnd,jdf->sjnf/dot_general | solution.py:30
  39.4 0.0 reduce-scatter.3.cloned.1.call-update
  39.5 0.0 reduce-scatter.5.cloned.1.call-start
  39.5 6.3 %fusion.9 = f32[4,2,64,1536]{3,2,0,1:T(8,128)} fusion(bf16[2,1024,1536]{2,1,0:T(8,128)(2,1)} %param.8, bf16[4,2,64,1024]{3,2,1,0:T(8,128)(2,1)S(1)} %all_to_all.10), kind=kOutput, calls=%fused_computation.10 | convolution fusion | flops 1610612736 | bytes 10485760 | tf_op jit(solution)/shard_map/sjnd,jdf->sjnf/dot_general | solution.py:31
  45.8 0.0 reduce-scatter.5.cloned.1.call-update
  45.8 0.0 all-gather.2.cloned.1.call-start
  45.9 54.4 %reduce-scatter.3.cloned.1.call-done = f32[4,2,64,384]{3,2,0,1:T(8,128)} async-done(((f32[4,2,64,1536]{3,2,0,1:T(8,128)}), f32[4,2,64,384]{3,2,0,1:T(8,128)}) %reduce-scatter.3.cloned.1.call-update) | async-done | bytes 786448 | tf_op jit(solution)/shard_map/reduce_scatter | solution.py:32
  100.3 62.6 %reduce-scatter.5.cloned.1.call-done = f32[4,2,64,384]{3,2,0,1:T(8,128)} async-done(((f32[4,2,64,1536]{3,2,0,1:T(8,128)}), f32[4,2,64,384]{3,2,0,1:T(8,128)}) %reduce-scatter.5.cloned.1.call-update) | async-done | bytes 786448 | tf_op jit(solution)/shard_map/reduce_scatter | solution.py:33
  163.0 2.3 multiply_convert_fusion
  165.3 0.0 all-gather.2.cloned.1.call-update
  165.3 0.0 copy-start.1
  165.3 36.7 %all-gather.2.cloned.1.call-done = bf16[4,2,64,1536]{3,2,0,1:T(8,128)(2,1)} async-done(((bf16[4,2,64,384]{3,2,0,1:T(8,128)(2,1)}), bf16[4,2,64,1536]{3,2,0,1:T(8,128)(2,1)}) %all-gather.2.cloned.1.call-update) | async-done | bytes 1572880 | tf_op jit(solution)/shard_map/all_gather | solution.py:35
  202.0 5.1 %fusion.16 = bf16[4,2,64,1024]{3,2,0,1:T(8,128)(2,1)S(1)} fusion(bf16[4,2,64,1536]{3,2,0,1:T(8,128)(2,1)} %all-gather.2.cloned.1.call-done, bf16[2,1536,1024]{2,1,0:T(8,128)(2,1)} %param.9), kind=kOutput, calls=%fused_computation.14 | convolution fusion | flops 1611137024 | bytes 8912896 | tf_op jit(solution)/shard_map/sjnf,jfd->sjnd/dot_general | solution.py:36
  207.1 1.1 copy.20
  208.1 3.5 %all-to-all-start.1 = ((bf16[4,2,64,1024]{3,2,1,0:T(8,128)(2,1)}), bf16[4,2,64,1024]{3,2,1,0:T(8,128)(2,1)S(1)}, u32[]{:S(2)}, u32[]{:S(2)}) async-start(bf16[4,2,64,1024]{3,2,1,0:T(8,128)(2,1)} %copy.20), calls=%async_computation.3 | async-start | bytes 2097152 | tf_op jit(solution)/shard_map/all_to_all | solution.py:38
  211.7 0.0 copy-done.1
  211.7 0.1 copy.21
  211.8 14.3 %all-to-all-done.1 = bf16[4,2,64,1024]{3,2,1,0:T(8,128)(2,1)S(1)} async-done(((bf16[4,2,64,1024]{3,2,1,0:T(8,128)(2,1)}), bf16[4,2,64,1024]{3,2,1,0:T(8,128)(2,1)S(1)}, u32[]{:S(2)}, u32[]{:S(2)}) %all-to-all-start.1) | async-done | bytes 1048608 | tf_op jit(solution)/shard_map/all_to_all | solution.py:38
  226.1 2.0 gather_fusion.1
  228.1 1.4 fusion.12
  (9 shorter events, 0.1 us)
Async XLA Ops:
  6.5 6.0 %copy-start = (bf16[64,1024]{1,0:T(8,128)(2,1)S(1)}, bf16[64,1024]{1,0:T(8,128)(2,1)}, u32[]{:S(2)}) copy-start(bf16[64,1024]{1,0:T(8,128)(2,1)} %param.6) | copy-start | bytes 393220
  6.5 93.8 %reduce-scatter.3.cloned.1.call-start = ((), (), s32[]{:S(2)}) async-start(), calls=%async_computation.4 | async-start | bytes 3932160 | tf_op jit(solution)/shard_map/reduce_scatter | solution.py:32
  39.5 123.5 %reduce-scatter.5.cloned.1.call-start = ((), (), s32[]{:S(2)}) async-start(), calls=%async_computation.5 | async-start | bytes 3932160 | tf_op jit(solution)/shard_map/reduce_scatter | solution.py:33
  45.8 156.2 %all-gather.2.cloned.1.call-start = ((), (), s32[]{:S(2)}) async-start(), calls=%async_computation.6 | async-start | bytes 1966080 | tf_op jit(solution)/shard_map/all_gather | solution.py:35
  165.3 46.3 %copy-start.1 = (f32[64,8]{0,1:T(8,128)S(1)}, f32[64,8]{0,1:T(8,128)}, u32[]{:S(2)}) copy-start(f32[64,8]{0,1:T(8,128)} %param.11) | copy-start | bytes 6148
  208.1 17.9 %all-to-all-start.1 = ((bf16[4,2,64,1024]{3,2,1,0:T(8,128)(2,1)}), bf16[4,2,64,1024]{3,2,1,0:T(8,128)(2,1)S(1)}, u32[]{:S(2)}, u32[]{:S(2)}) async-start(bf16[4,2,64,1024]{3,2,1,0:T(8,128)(2,1)} %copy.20), calls=%async_computation.3 | async-start | bytes 2097152 | tf_op jit(solution)/shard_map/all_to_all | solution.py:38
Sparse Core Ops, SparseCore 0:
  39.6 60.6 reduce-scatter.2
  102.6 60.3 reduce-scatter.4
  165.4 36.5 all-gather.1
where the time goes:
time: 236 us
  waiting for transfers between devices  168 us (71%)
  blocking collectives  18.5 us (8%)
  matrix products  17.6 us (7%)
  between operations  13.2 us (6%)
  local copies, waits for them, and re-layouts  9.18 us (4%)
  other arithmetic  5.83 us (2%)
  starting transfers between devices  3.6 us (2%)
    reduce_scatter x1, waiting for transfers between devices, per_device(): lax.psum_scatter(up_part, 'tensor', scatter_dimension=3, tiled=True)  62.6 us
    reduce_scatter x1, waiting for transfers between devices, per_device(): lax.psum_scatter(gate_part, 'tensor', scatter_dimension=3, tiled=True)  54.4 us
    all_gather x1, waiting for transfers between devices, per_device(): hidden = lax.all_gather(hidden_share, 'tensor', axis=3, tiled=True)  36.7 us
    all_to_all x1, blocking collectives, per_device(): lax.all_to_all(outgoing, 'expert', split_axis=0, concat_axis=0, tiled=True)  18.5 us
    all_to_all x1, waiting for transfers between devices, per_device(): lax.all_to_all(returned, 'expert', split_axis=0, concat_axis=0, tiled=True)  14.3 us
    dot_general x1, matrix products, per_device(): jnp.einsum('sjnd,jdf->sjnf', received, w_up, preferred_element_type=jnp.f...  6.3 us
    dot_general x1, matrix products, per_device(): jnp.einsum('sjnd,jdf->sjnf', received, w_gate, preferred_element_type=jnp...  6.27 us
    dot_general x1, matrix products, per_device(): jnp.einsum('sjnf,jfd->sjnd', hidden, w_down, preferred_element_type=jnp.f...  5.06 us
  transfers between devices with their start and end apart: 4, of which 4 were waited for; matrix products, arithmetic and copies ran while one was open for 3% of the time, Pallas kernels for 0%

commit v1 on v0

--- a/solution.py
+++ b/solution.py
@@ -32,8 +32,28 @@
     gate_share = lax.psum_scatter(gate_part, "tensor", scatter_dimension=3, tiled=True)
     up_share = lax.psum_scatter(up_part, "tensor", scatter_dimension=3, tiled=True)
     hidden_share = (jax.nn.silu(gate_share) * up_share).astype(jnp.bfloat16)
-    hidden = lax.all_gather(hidden_share, "tensor", axis=3, tiled=True)
-    result = jnp.einsum("sjnf,jfd->sjnd", hidden, w_down, preferred_element_type=jnp.float32)
+    current_arr, wide_out = (lax.axis_size("tensor"), lax.axis_index("tensor"))
+    by_place = [(c, (c - 1) % current_arr) for c in range(current_arr)]
+    odd = hidden_share.shape[3]
+    finding = hidden_share
+    result = jnp.einsum(
+        "sjnf,jfd->sjnd",
+        finding,
+        lax.dynamic_slice_in_dim(w_down, wide_out * odd, finding.shape[3], axis=1),
+        preferred_element_type=jnp.float32,
+    )
+    nth = 1
+    while nth < current_arr:
+        finding = lax.ppermute(finding, "tensor", by_place)
+        result = result + jnp.einsum(
+            "sjnf,jfd->sjnd",
+            finding,
+            lax.dynamic_slice_in_dim(
+                w_down, (wide_out + nth) % current_arr * odd, finding.shape[3], axis=1
+            ),
+            preferred_element_type=jnp.float32,
+        )
+        nth += 1
     returned = result.astype(jnp.bfloat16)
     combined = lax.all_to_all(returned, "expert", split_axis=0, concat_axis=0, tiled=True).reshape(
         experts_all * capacity, col_share

time: 236 us -> 229 us (0.970)
  waiting for transfers between devices: 168 us -> 149 us
  starting transfers between devices: 3.6 us -> 14.1 us
    all_gather x1 -> x0, waiting for transfers between devices: 36.7 us -> none  [per_device(): hidden = lax.all_gather(hidden_share, 'tensor', axis=3, tiled=True)]
    ppermute x0 -> x3, waiting for transfers between devices: none -> 17.8 us  [per_device(): finding = lax.ppermute(finding, 'tensor', by_place)]
    ppermute x0 -> x3, starting transfers between devices: none -> 10.6 us  [per_device(): finding = lax.ppermute(finding, 'tensor', by_place)]
    dot_general x1 -> x4, matrix products: 5.06 us -> 5.89 us  [the longest x3 3.62 us: per_device(): jnp.einsum('sjnf,jfd->sjnd', finding, lax.dynamic_slice_in_dim(w_down, (w...]
  transfers between devices with their start and end apart: 4 -> 6, of which waited for: 4 -> 6; matrix products, arithmetic and copies ran while one was open for 3% -> 5% of each run, Pallas kernels for 0% -> 0%
where the time goes in v1:
time: 229 us; the launch traced here: 228 us
  waiting for transfers between devices  149 us (65%)
  blocking collectives  18.5 us (8%)
  matrix products  18.4 us (8%)
  starting transfers between devices  14.1 us (6%)
  between operations  13.6 us (6%)
  local copies, waits for them, and re-layouts  9.21 us (4%)
  other arithmetic  5.23 us (2%)
    reduce_scatter x1, waiting for transfers between devices, per_device(): lax.psum_scatter(up_part, 'tensor', scatter_dimension=3, tiled=True)  62.6 us
    reduce_scatter x1, waiting for transfers between devices, per_device(): lax.psum_scatter(gate_part, 'tensor', scatter_dimension=3, tiled=True)  54.5 us
    all_to_all x1, blocking collectives, per_device(): lax.all_to_all(outgoing, 'expert', split_axis=0, concat_axis=0, tiled=True)  18.5 us
    ppermute x3, waiting for transfers between devices, per_device(): finding = lax.ppermute(finding, 'tensor', by_place)  17.8 us
    all_to_all x1, waiting for transfers between devices, per_device(): lax.all_to_all(returned, 'expert', split_axis=0, concat_axis=0, tiled=True)  14.3 us
    ppermute x3, starting transfers between devices, per_device(): finding = lax.ppermute(finding, 'tensor', by_place)  10.6 us
    dot_general x1, matrix products, per_device(): jnp.einsum('sjnd,jdf->sjnf', received, w_up, preferred_element_type=jnp.f...  6.28 us
    dot_general x1, matrix products, per_device(): jnp.einsum('sjnd,jdf->sjnf', received, w_gate, preferred_element_type=jnp...  6.24 us
  transfers between devices with their start and end apart: 6, of which 6 were waited for; matrix products, arithmetic and copies ran while one was open for 5% of the time, Pallas kernels for 0%

profile of v1, /device:TPU:0, one launch (start us, length us, event | category | flops | bytes accessed | tf_op | source)
XLA Modules:
  0.0 228.3 jit_solution(15617010850192639946)
XLA Ops:
  6.5 0.0 copy-start
  6.5 0.0 reduce-scatter.3.cloned.1.call-start
  6.5 0.8 copy.16
  7.3 0.1 eq.33
  7.4 0.1 eq.29
  7.5 0.7 broadcast_multiply_fusion
  8.2 1.1 reduce-window.6
  9.4 0.2 slice_reduce_fusion
  9.6 0.1 copy.15
  9.7 0.1 mul.45
  9.8 0.1 fusion.28
  9.9 2.4 %scatter_custom_fusion = s32[512]{0:T(512)S(1)} fusion(s32[512]{0:T(512)S(1)} %bitcast.65, s32[512]{0:T(512)S(1)} %add_select_fusion, s32[]{:T(128)} %constant.57.clone.1), kind=kCustom, calls=%fused_computation.48 | custom fusion | bytes 2052 | tf_op jit(solution)/shard_map/scatter | solution.py:25
  12.4 0.1 broadcast_in_dim.26
  12.5 0.0 copy-done
  12.5 2.1 gather_fusion
  14.5 0.1 broadcast_select_fusion
  14.7 18.5 %all_to_all.10 = bf16[4,2,64,1024]{3,2,1,0:T(8,128)(2,1)S(1)} all-to-all(bf16[4,2,64,1024]{3,2,1,0:T(8,128)(2,1)S(1)} %broadcast_select_fusion), channel_id=1, replica_groups=mesh['group'=2,'expert'=4,'tensor'=4] {'expert'}, dimensions={0} | all-to-all | bytes 2097152 | tf_op jit(solution)/shard_map/all_to_all | solution.py:29
  33.2 6.2 %fusion.4 = f32[4,2,64,1536]{3,2,0,1:T(8,128)} fusion(bf16[2,1024,1536]{2,1,0:T(8,128)(2,1)} %param.7, bf16[4,2,64,1024]{3,2,1,0:T(8,128)(2,1)S(1)} %all_to_all.10), kind=kOutput, calls=%fused_computation.7 | convolution fusion | flops 1610612736 | bytes 10485760 | tf_op jit(solution)/shard_map/sjnd,jdf->sjnf/dot_general | solution.py:30
  39.4 0.0 reduce-scatter.3.cloned.1.call-update
  39.4 0.0 reduce-scatter.5.cloned.1.call-start
  39.5 6.3 %fusion.7 = f32[4,2,64,1536]{3,2,0,1:T(8,128)} fusion(bf16[2,1024,1536]{2,1,0:T(8,128)(2,1)} %param.8, bf16[4,2,64,1024]{3,2,1,0:T(8,128)(2,1)S(1)} %all_to_all.10), kind=kOutput, calls=%fused_computation.8 | convolution fusion | flops 1610612736 | bytes 10485760 | tf_op jit(solution)/shard_map/sjnd,jdf->sjnf/dot_general | solution.py:31
  45.8 0.0 reduce-scatter.5.cloned.1.call-update
  45.8 54.5 %reduce-scatter.3.cloned.1.call-done = f32[4,2,64,384]{3,2,0,1:T(8,128)} async-done(((f32[4,2,64,1536]{3,2,0,1:T(8,128)}), f32[4,2,64,384]{3,2,0,1:T(8,128)}) %reduce-scatter.3.cloned.1.call-update) | async-done | bytes 786448 | tf_op jit(solution)/shard_map/reduce_scatter | solution.py:32
  100.3 62.6 %reduce-scatter.5.cloned.1.call-done = f32[4,2,64,384]{3,2,0,1:T(8,128)} async-done(((f32[4,2,64,1536]{3,2,0,1:T(8,128)}), f32[4,2,64,384]{3,2,0,1:T(8,128)}) %reduce-scatter.5.cloned.1.call-update) | async-done | bytes 786448 | tf_op jit(solution)/shard_map/reduce_scatter | solution.py:33
  163.0 0.0 slice-start
  163.0 1.7 multiply_convert_fusion
  164.7 2.0 collective-permute-start
  166.7 8.5 %collective-permute-done = bf16[4,2,64,384]{3,2,0,1:T(8,128)(2,1)S(1)} collective-permute-done((bf16[4,2,64,384]{3,2,0,1:T(8,128)(2,1)S(1)}, bf16[4,2,64,384]{3,2,0,1:T(8,128)(2,1)S(1)}, u32[]{:S(2)}, u32[]{:S(2)}) %collective-permute-start) | collective-permute-done | bytes 393248 | tf_op jit(solution)/shard_map/ppermute | solution.py:47
  175.3 4.3 %collective-permute-start.1 = (bf16[4,2,64,384]{3,2,0,1:T(8,128)(2,1)S(1)}, bf16[4,2,64,384]{3,2,0,1:T(8,128)(2,1)S(1)}, u32[]{:S(2)}, u32[]{:S(2)}) collective-permute-start(bf16[4,2,64,384]{3,2,0,1:T(8,128)(2,1)S(1)} %collective-permute-done), channel_id=1, source_target_pairs={{0,3},{1,0},{2,1},{3,2},{4,7},{5,4},{6,5},{7,6},{8,11},{9,8},{10,9... | collective-permute-start | bytes 1179656 | tf_op jit(solution)/shard_map/ppermute | solution.py:47
  179.5 0.0 slice-start.1
  179.5 2.3 fusion.16
  181.8 5.4 %collective-permute-done.1 = bf16[4,2,64,384]{3,2,0,1:T(8,128)(2,1)S(1)} collective-permute-done((bf16[4,2,64,384]{3,2,0,1:T(8,128)(2,1)S(1)}, bf16[4,2,64,384]{3,2,0,1:T(8,128)(2,1)S(1)}, u32[]{:S(2)}, u32[]{:S(2)}) %collective-permute-start.1) | collective-permute-done | bytes 393248 | tf_op jit(solution)/shard_map/ppermute | solution.py:47
  187.2 4.3 %collective-permute-start.2 = (bf16[4,2,64,384]{3,2,0,1:T(8,128)(2,1)S(1)}, bf16[4,2,64,384]{3,2,0,1:T(8,128)(2,1)S(1)}, u32[]{:S(2)}, u32[]{:S(2)}) collective-permute-start(bf16[4,2,64,384]{3,2,0,1:T(8,128)(2,1)S(1)} %collective-permute-done.1), channel_id=1, source_target_pairs={{0,3},{1,0},{2,1},{3,2},{4,7},{5,4},{6,5},{7,6},{8,11},{9,8},{10,9... | collective-permute-start | bytes 1179656 | tf_op jit(solution)/shard_map/ppermute | solution.py:47
  191.5 2.1 fusion.14
  193.6 0.0 slice-done
  193.6 0.0 slice-done.1
  193.6 0.7 fusion.12
  194.4 3.9 %collective-permute-done.2 = bf16[4,2,64,384]{3,2,0,1:T(8,128)(2,1)S(1)} collective-permute-done((bf16[4,2,64,384]{3,2,0,1:T(8,128)(2,1)S(1)}, bf16[4,2,64,384]{3,2,0,1:T(8,128)(2,1)S(1)}, u32[]{:S(2)}, u32[]{:S(2)}) %collective-permute-start.2) | collective-permute-done | bytes 393248 | tf_op jit(solution)/shard_map/ppermute | solution.py:47
  198.3 0.8 fusion.22
  199.1 0.0 copy-start.1
  199.1 1.1 copy.20
  200.2 3.5 %all-to-all-start.1 = ((bf16[4,2,64,1024]{3,2,1,0:T(8,128)(2,1)}), bf16[4,2,64,1024]{3,2,1,0:T(8,128)(2,1)S(1)}, u32[]{:S(2)}, u32[]{:S(2)}) async-start(bf16[4,2,64,1024]{3,2,1,0:T(8,128)(2,1)} %copy.20), calls=%async_computation.3 | async-start | bytes 2097152 | tf_op jit(solution)/shard_map/all_to_all | solution.py:58
  203.7 0.0 copy-done.1
  203.7 0.1 copy.21
  203.8 14.3 %all-to-all-done.1 = bf16[4,2,64,1024]{3,2,1,0:T(8,128)(2,1)S(1)} async-done(((bf16[4,2,64,1024]{3,2,1,0:T(8,128)(2,1)}), bf16[4,2,64,1024]{3,2,1,0:T(8,128)(2,1)S(1)}, u32[]{:S(2)}, u32[]{:S(2)}) %all-to-all-start.1) | async-done | bytes 1048608 | tf_op jit(solution)/shard_map/all_to_all | solution.py:58
  218.1 2.0 gather_fusion.1
  220.2 1.3 fusion.10
  (10 shorter events, 0.1 us)
Async XLA Ops:
  6.5 6.0 %copy-start = (bf16[64,1024]{1,0:T(8,128)(2,1)S(1)}, bf16[64,1024]{1,0:T(8,128)(2,1)}, u32[]{:S(2)}) copy-start(bf16[64,1024]{1,0:T(8,128)(2,1)} %param.6) | copy-start | bytes 393220
  6.5 93.8 %reduce-scatter.3.cloned.1.call-start = ((), (), s32[]{:S(2)}) async-start(), calls=%async_computation.4 | async-start | bytes 3932160 | tf_op jit(solution)/shard_map/reduce_scatter | solution.py:32
  39.4 123.5 %reduce-scatter.5.cloned.1.call-start = ((), (), s32[]{:S(2)}) async-start(), calls=%async_computation.5 | async-start | bytes 3932160 | tf_op jit(solution)/shard_map/reduce_scatter | solution.py:33
  163.0 30.6 %slice-start = ((s8[6291456]{0:T(1024)(128)(4,1)}), s8[2097152]{0:T(1024)(128)(4,1)S(1)}, s32[]{:S(2)}) async-start(s8[6291456]{0:T(1024)(128)(4,1)} %bitcast.62), calls=%async_computation.6 | async-start | bytes 4194304
  164.7 10.5 %collective-permute-start = (bf16[4,2,64,384]{3,2,0,1:T(8,128)(2,1)S(1)}, bf16[4,2,64,384]{3,2,0,1:T(8,128)(2,1)S(1)}, u32[]{:S(2)}, u32[]{:S(2)}) collective-permute-start(bf16[4,2,64,384]{3,2,0,1:T(8,128)(2,1)S(1)} %multiply_convert_fusion), channel_id=1, source_target_pairs={{0,3},{1,0},{2,1},{3,2},{4,7},{5,4},{6,5},{7,6},{8,11},{9,8},{10,9... | collective-permute-start | bytes 1179656 | tf_op jit(solution)/shard_map/ppermute | solution.py:47
  175.3 11.9 %collective-permute-start.1 = (bf16[4,2,64,384]{3,2,0,1:T(8,128)(2,1)S(1)}, bf16[4,2,64,384]{3,2,0,1:T(8,128)(2,1)S(1)}, u32[]{:S(2)}, u32[]{:S(2)}) collective-permute-start(bf16[4,2,64,384]{3,2,0,1:T(8,128)(2,1)S(1)} %collective-permute-done), channel_id=1, source_target_pairs={{0,3},{1,0},{2,1},{3,2},{4,7},{5,4},{6,5},{7,6},{8,11},{9,8},{10,9... | collective-permute-start | bytes 1179656 | tf_op jit(solution)/shard_map/ppermute | solution.py:47
  179.5 14.1 %slice-start.1 = ((s8[6291456]{0:T(1024)(128)(4,1)}), s8[4194304]{0:T(1024)(128)(4,1)S(1)}, s32[]{:S(2)}) async-start(s8[6291456]{0:T(1024)(128)(4,1)} %bitcast.62), calls=%async_computation.7 | async-start | bytes 8388608
  187.2 11.1 %collective-permute-start.2 = (bf16[4,2,64,384]{3,2,0,1:T(8,128)(2,1)S(1)}, bf16[4,2,64,384]{3,2,0,1:T(8,128)(2,1)S(1)}, u32[]{:S(2)}, u32[]{:S(2)}) collective-permute-start(bf16[4,2,64,384]{3,2,0,1:T(8,128)(2,1)S(1)} %collective-permute-done.1), channel_id=1, source_target_pairs={{0,3},{1,0},{2,1},{3,2},{4,7},{5,4},{6,5},{7,6},{8,11},{9,8},{10,9... | collective-permute-start | bytes 1179656 | tf_op jit(solution)/shard_map/ppermute | solution.py:47
  199.1 4.6 %copy-start.1 = (f32[64,8]{0,1:T(8,128)S(1)}, f32[64,8]{0,1:T(8,128)}, u32[]{:S(2)}) copy-start(f32[64,8]{0,1:T(8,128)} %param.11) | copy-start | bytes 6148
  200.2 17.9 %all-to-all-start.1 = ((bf16[4,2,64,1024]{3,2,1,0:T(8,128)(2,1)}), bf16[4,2,64,1024]{3,2,1,0:T(8,128)(2,1)S(1)}, u32[]{:S(2)}, u32[]{:S(2)}) async-start(bf16[4,2,64,1024]{3,2,1,0:T(8,128)(2,1)} %copy.20), calls=%async_computation.3 | async-start | bytes 2097152 | tf_op jit(solution)/shard_map/all_to_all | solution.py:58
Sparse Core Ops, SparseCore 0:
  39.6 60.7 reduce-scatter.2
  102.6 60.3 reduce-scatter.4
